TPU v7x, 16 devices: a whole 2x2x2 slice. The times are simulated.
16 devices in a mesh: dp: 2 (over z), ep: 8 (over y, x, core).
Axes of the slice: x: 2, y: 2, z: 2, core: 2. Of those that a mesh axis runs over, the one named last changes fastest.
Arguments:
- x_in: bfloat16 [8192, 4096], P(('dp', 'ep'))
- ln_gain: float32 [4096], replicated
- ln_bias: float32 [4096], replicated
- w_router: bfloat16 [4096, 16], replicated
- w_gate: bfloat16 [16, 4096, 960], P('ep')
- w_up: bfloat16 [16, 4096, 960], P('ep')
- w_down: bfloat16 [16, 960, 4096], P('ep')
- expert_ids: int32 [8192, 2], P(('dp', 'ep'))
- slot_ids: int32 [8192, 2], P(('dp', 'ep'))
- d_out: bfloat16 [8192, 4096], P(('dp', 'ep'))
Outputs:
- output 1: bfloat16 [8192, 4096], P(('dp', 'ep'))
- output 2: bfloat16 [8192, 4096], P(('dp', 'ep'))
- output 3: float32 [4096], replicated
- output 4: float32 [4096], replicated
- output 5: float32 [4096, 16], replicated
- output 6: float32 [16, 4096, 960], P('ep')
- output 7: float32 [16, 4096, 960], P('ep')
- output 8: float32 [16, 960, 4096], P('ep')
All inputs are finite; a program needn't handle non-finite values.
Results may differ from a plain program's by a relative error of at most 0.00544038.
Values are sent between devices in bfloat16 or wider.
A program may use at most 1 GiB of HBM per device.

v0:
```python
import jax
import jax.numpy as jnp
from jax import lax
from jax.sharding import PartitionSpec as P

LN_EPS = 1e-5


def capacity_for(tokens_dev, experts, n_top):
    return 8 * ((5 * tokens_dev * n_top + 32 * experts - 1) // (32 * experts))


def norm_forward(x_loc, ln_gain, ln_bias):
    x_f = x_loc.astype(jnp.float32)
    mean_x = jnp.mean(x_f, axis=-1, keepdims=True)
    centered = x_f - mean_x
    var_x = jnp.mean(centered * centered, axis=-1, keepdims=True)
    inv_std = lax.rsqrt(var_x + LN_EPS)
    normed = centered * inv_std
    hidden = (normed * ln_gain + ln_bias).astype(jnp.bfloat16)
    return x_f, hidden, normed, inv_std


def norm_backward(d_hidden, normed, inv_std, ln_gain):
    d_normed = d_hidden * ln_gain
    mean_dn = jnp.mean(d_normed, axis=-1, keepdims=True)
    mean_dnn = jnp.mean(d_normed * normed, axis=-1, keepdims=True)
    return inv_std * (d_normed - mean_dn - normed * mean_dnn)


def router_forward(hidden, w_router, ids_loc):
    experts = w_router.shape[1]
    logits = jnp.dot(hidden, w_router, preferred_element_type=jnp.float32)
    pick_mask = (ids_loc[..., None] == jnp.arange(experts)).astype(jnp.float32)
    chosen = jnp.sum(pick_mask * logits[..., None, :], axis=-1)
    return jax.nn.softmax(chosen, axis=-1), pick_mask


def router_backward(gate_probs, pick_mask, pair_out, dout_f):
    d_gates = jnp.sum(pair_out * dout_f[:, None, :], axis=-1)
    d_chosen = gate_probs * (d_gates - jnp.sum(gate_probs * d_gates, axis=-1, keepdims=True))
    return jnp.sum(d_chosen[..., None] * pick_mask, axis=-2)


def expert_forward(expert_in, gate_loc, up_loc, down_loc):
    pre_gate = jnp.einsum("erm,emf->erf", expert_in, gate_loc, preferred_element_type=jnp.float32).astype(jnp.bfloat16)
    pre_up = jnp.einsum("erm,emf->erf", expert_in, up_loc, preferred_element_type=jnp.float32).astype(jnp.bfloat16)
    gate_f = pre_gate.astype(jnp.float32)
    act_mix = (gate_f * jax.nn.sigmoid(gate_f) * pre_up.astype(jnp.float32)).astype(jnp.bfloat16)
    expert_out = jnp.einsum("erf,efm->erm", act_mix, down_loc, preferred_element_type=jnp.float32).astype(jnp.bfloat16)
    return expert_out, (pre_gate, pre_up, act_mix)


def expert_backward(expert_in, saved, grad_in, gate_loc, up_loc, down_loc):
    pre_gate, pre_up, act_mix = saved
    d_mix = jnp.einsum("erm,efm->erf", grad_in, down_loc, preferred_element_type=jnp.float32).astype(jnp.bfloat16).astype(jnp.float32)
    grad_down = jnp.einsum("erf,erm->efm", act_mix, grad_in, preferred_element_type=jnp.float32)
    gate_f = pre_gate.astype(jnp.float32)
    sig_gate = jax.nn.sigmoid(gate_f)
    up_f = pre_up.astype(jnp.float32)
    d_pre_gate = (d_mix * up_f * sig_gate * (1.0 + gate_f * (1.0 - sig_gate))).astype(jnp.bfloat16)
    d_pre_up = (d_mix * gate_f * sig_gate).astype(jnp.bfloat16)
    grad_gate = jnp.einsum("erm,erf->emf", expert_in, d_pre_gate, preferred_element_type=jnp.float32)
    grad_up = jnp.einsum("erm,erf->emf", expert_in, d_pre_up, preferred_element_type=jnp.float32)
    d_expert_in = (jnp.einsum("erf,emf->erm", d_pre_gate, gate_loc, preferred_element_type=jnp.float32) + jnp.einsum("erf,emf->erm", d_pre_up, up_loc, preferred_element_type=jnp.float32)).astype(jnp.bfloat16)
    return d_expert_in, grad_gate, grad_up, grad_down


def solution(mesh):
    n_ep = mesh.shape["ep"]
    tok_spec = P(("dp", "ep"), None)
    exp_spec = P("ep", None, None)

    def local_step(x_loc, ln_gain, ln_bias, w_router, gate_loc, up_loc, down_loc, ids_loc, slots_loc, dout_loc):
        tokens_dev, model_dim = x_loc.shape
        experts = w_router.shape[1]
        local_exp = gate_loc.shape[0]
        n_top = ids_loc.shape[1]
        capacity = capacity_for(tokens_dev, experts, n_top)
        x_f, hidden, normed, inv_std = norm_forward(x_loc, ln_gain, ln_bias)
        gate_probs, pick_mask = router_forward(hidden, w_router, ids_loc)
        target = jnp.where(slots_loc >= 0, ids_loc * capacity + slots_loc, -1)
        pair_hot = (target[..., None] == jnp.arange(experts * capacity)).astype(jnp.bfloat16)
        token_hot = jnp.sum(pair_hot, axis=1)
        send_rows = jnp.einsum("ts,tm->sm", token_hot, hidden, preferred_element_type=jnp.float32).astype(jnp.bfloat16)
        expert_in = lax.all_to_all(send_rows.reshape(n_ep, local_exp, capacity, model_dim), "ep", 0, 2, tiled=True)
        expert_in = expert_in.reshape(local_exp, n_ep * capacity, model_dim)
        expert_out, saved = expert_forward(expert_in, gate_loc, up_loc, down_loc)
        ret_rows = lax.all_to_all(expert_out.reshape(1, local_exp, n_ep * capacity, model_dim), "ep", 2, 0, tiled=True)
        ret_rows = ret_rows.reshape(experts * capacity, model_dim)
        pair_out = jnp.dot(pair_hot.reshape(tokens_dev * n_top, experts * capacity), ret_rows, preferred_element_type=jnp.float32).reshape(tokens_dev, n_top, model_dim)
        mixed = jnp.sum(gate_probs[..., None] * pair_out, axis=1)
        moe_out = (x_f + mixed).astype(jnp.bfloat16)
        dout_f = dout_loc.astype(jnp.float32)
        d_logits = router_backward(gate_probs, pick_mask, pair_out, dout_f)
        pair_grad = (gate_probs[..., None] * dout_f[:, None, :]).astype(jnp.bfloat16)
        send_grad = jnp.einsum("tks,tkm->sm", pair_hot, pair_grad, preferred_element_type=jnp.float32).astype(jnp.bfloat16)
        grad_in = lax.all_to_all(send_grad.reshape(n_ep, local_exp, capacity, model_dim), "ep", 0, 2, tiled=True)
        grad_in = grad_in.reshape(local_exp, n_ep * capacity, model_dim)
        d_expert_in, grad_gate, grad_up, grad_down = expert_backward(expert_in, saved, grad_in, gate_loc, up_loc, down_loc)
        d_rows = lax.all_to_all(d_expert_in.reshape(1, local_exp, n_ep * capacity, model_dim), "ep", 2, 0, tiled=True)
        d_rows = d_rows.reshape(experts * capacity, model_dim)
        d_hidden_moe = jnp.einsum("ts,sm->tm", token_hot, d_rows, preferred_element_type=jnp.float32)
        d_hidden_router = jnp.einsum("te,me->tm", d_logits, w_router, preferred_element_type=jnp.float32)
        d_hidden = (d_hidden_moe + d_hidden_router).astype(jnp.bfloat16).astype(jnp.float32)
        grad_x = (dout_f + norm_backward(d_hidden, normed, inv_std, ln_gain)).astype(jnp.bfloat16)
        small_sums = lax.psum((jnp.sum(d_hidden * normed, axis=0), jnp.sum(d_hidden, axis=0), jnp.einsum("tm,te->me", hidden, d_logits, preferred_element_type=jnp.float32)), ("dp", "ep"))
        expert_sums = lax.psum((grad_gate, grad_up, grad_down), "dp")
        return (moe_out, grad_x) + tuple(small_sums) + tuple(expert_sums)

    return jax.shard_map(local_step, mesh=mesh, in_specs=(tok_spec, P(None), P(None), P(None, None), exp_spec, exp_spec, exp_spec, tok_spec, tok_spec, tok_spec), out_specs=(tok_spec, tok_spec, P(None), P(None), P(None, None), exp_spec, exp_spec, exp_spec), check_vma=False)
```

profile of v0, /device:TPU:0, one launch (start us, length us, event | category | flops | bytes accessed | tf_op | source)
XLA Modules:
  0.0 2603.3 jit_solution(9462380173714716266)
XLA Ops:
  7.2 3.0 convert_reduce_fusion.1
  10.2 0.5 copy-done.1
  10.7 1.2 fusion.14
  12.0 1.2 fusion.34
  13.3 2.3 fusion.9
  15.6 8.2 convolution_convert_fusion
  23.8 5.5 all-to-all-start
  29.2 6.6 convert_element_type.82
  35.9 1.2 fusion.49
  37.2 0.6 copy-done.18
  37.8 0.6 copy-done.28
  38.4 15.1 bitcast_convert_fusion
  53.5 92.9 %all-to-all-done = bf16[8,2,80,4096]{3,2,1,0:T(8,128)(2,1)} async-done(((bf16[8,2,80,4096]{3,2,1,0:T(8,128)(2,1)}), bf16[8,2,80,4096]{3,2,1,0:T(8,128)(2,1)}, u32[]{:S(2)}, u32[]{:S(2)}) %all-to-all-start) | async-done | bytes 10485792 | tf_op jit(solution)/shard_map/all_to_all | solution.py:86
  146.4 5.4 all-to-all-start.2
  151.8 9.6 copy.49
  161.4 18.3 convolution_convert_fusion.3
  179.7 20.0 convolution_convert_fusion.2
  199.7 18.7 convert_bitcast_fusion
  218.4 20.0 copy.50
  238.4 29.8 %all-to-all-done.2 = bf16[8,2,80,4096]{3,2,1,0:T(8,128)(2,1)} async-done(((bf16[8,2,80,4096]{3,2,1,0:T(8,128)(2,1)}), bf16[8,2,80,4096]{3,2,1,0:T(8,128)(2,1)}, u32[]{:S(2)}, u32[]{:S(2)}) %all-to-all-start.2) | async-done | bytes 10485792 | tf_op jit(solution)/shard_map/all_to_all | solution.py:98
  268.2 5.1 all-to-all-start.1
  273.4 0.0 all-reduce.5.cloned.1.call-start
  273.4 9.7 copy.52
  283.2 19.3 convolution_convert_fusion.1
  302.5 23.0 fusion.42
  325.5 24.4 fusion.45
  350.0 39.9 %all-to-all-done.1 = bf16[1,2,640,4096]{3,1,0,2:T(2,128)(2,1)} async-done(((bf16[1,2,640,4096]{3,1,0,2:T(2,128)(2,1)}), bf16[1,2,640,4096]{3,1,0,2:T(2,128)(2,1)}, u32[]{:S(2)}, u32[]{:S(2)}) %all-to-all-start.1) | async-done | bytes 10485792 | tf_op jit(solution)/shard_map/all_to_all | solution.py:89
  389.9 15.7 copy.51
  405.6 20.3 multiply_reduce_fusion
  426.0 1.4 fusion.51
  427.4 0.0 all-reduce.7.cloned.1.call-start
  427.4 23.5 fusion.39
  450.9 1.7 copy-done.7
  452.6 21.6 fusion.47
  474.3 22.2 fusion.3
  496.5 17.9 copy.53
  514.4 119.9 %all_to_all.60 = bf16[1,2,640,4096]{3,1,0,2:T(2,128)(2,1)} all-to-all(bf16[1,2,640,4096]{3,1,0,2:T(2,128)(2,1)S(1)} %copy.53), channel_id=1, replica_groups=mesh['dp'=2,'ep'=8] {'ep'}, dimensions={2} | all-to-all | bytes 20971520 | tf_op jit(solution)/shard_map/all_to_all | solution.py:101
  634.2 15.4 copy.54
  649.7 9.7 copy.55
  659.4 8.8 fusion.50
  668.3 5.7 fusion.17
  673.9 34.2 %all-reduce = (f32[4096]{0:T(1024)}, f32[4096]{0:T(1024)}) all-reduce(f32[4096]{0:T(1024)S(1)} %get-tuple-element.10, f32[4096]{0:T(1024)S(1)} %get-tuple-element.13), channel_id=1, replica_groups=mesh['dp'=2,'ep'=8] {'dp','ep'}, use_global_device_ids=true, to_apply=%region_13.14 | all-reduce | flops 8192 | bytes 65536 | tf_op jit(solution)/shard_map/psum | solution.py:107
  708.1 11.6 fusion.13
  719.7 1813.5 %all-reduce.7.cloned.1.call-done = (f32[2,4096,960]{1,2,0:T(8,128)}, f32[2,4096,960]{1,2,0:T(8,128)}, f32[2,960,4096]{2,1,0:T(8,128)}) async-done(((f32[2,4096,960]{1,2,0:T(8,128)}, f32[2,4096,960]{1,2,0:T(8,128)}, f32[2,960,4096]{2,1,0:T(8,128)}), (f32[2,4096,960]{1,2,0:T(8,128)}, f32[2,4096,960]{1,2,0:T(8,128)}, f32[2,960,4096]{2,1,0:T(8,128)})) %all-reduce.7.cloned.1.call-update) | async-done | bytes 94371856 | tf_op jit(solution)/shard_map/psum | solution.py:108
  2533.2 1.7 copy.60
  2534.9 25.1 copy.61
  2560.0 25.0 copy.62
  2585.1 11.0 copy.63
  (87 shorter events, 0.4 us)
Async XLA Ops:
  7.2 28.7 %copy-start = (bf16[4096,16]{0,1:T(8,128)(2,1)S(1)}, bf16[4096,16]{0,1:T(8,128)(2,1)}, u32[]{:S(2)}) copy-start(bf16[4096,16]{0,1:T(8,128)(2,1)} %param.13) | copy-start | bytes 393220
  7.2 3.5 copy-start.1
  7.2 4.7 copy-start.16
  7.2 4.7 copy-start.27
  7.2 6.0 copy-start.12
  7.2 6.0 copy-start.24
  10.7 2.5 copy-start.20
  11.9 1.3 copy-start.22
  12.0 25.8 copy-start.25
  13.2 10.5 copy-start.8
  15.6 8.2 copy-start.3
  23.8 122.6 %all-to-all-start = ((bf16[8,2,80,4096]{3,2,1,0:T(8,128)(2,1)}), bf16[8,2,80,4096]{3,2,1,0:T(8,128)(2,1)}, u32[]{:S(2)}, u32[]{:S(2)}) async-start(bf16[8,2,80,4096]{3,2,1,0:T(8,128)(2,1)} %bitcast.62), calls=%async_computation | async-start | bytes 20971520 | tf_op jit(solution)/shard_map/all_to_all | solution.py:86
  29.2 6.6 copy-start.4
  37.1 16.4 copy-start.10
  37.1 16.3 copy-start.14
  37.2 0.6 copy-start.18
  37.8 0.6 copy-start.28
  146.4 121.9 %all-to-all-start.2 = ((bf16[8,2,80,4096]{3,2,1,0:T(8,128)(2,1)}), bf16[8,2,80,4096]{3,2,1,0:T(8,128)(2,1)}, u32[]{:S(2)}, u32[]{:S(2)}) async-start(bf16[8,2,80,4096]{3,2,1,0:T(8,128)(2,1)} %bitcast.61), calls=%async_computation.2 | async-start | bytes 20971520 | tf_op jit(solution)/shard_map/all_to_all | solution.py:98
  179.6 145.9 %copy-start.6 = (bf16[2,640,960]{1,2,0:T(8,128)(2,1)}, bf16[2,640,960]{1,2,0:T(8,128)(2,1)S(1)}, u32[]{:S(2)}) copy-start(bf16[2,640,960]{1,2,0:T(8,128)(2,1)S(1)} %convolution_convert_fusion.3) | copy-start | bytes 7372804
  268.2 121.6 %all-to-all-start.1 = ((bf16[1,2,640,4096]{3,1,0,2:T(2,128)(2,1)}), bf16[1,2,640,4096]{3,1,0,2:T(2,128)(2,1)}, u32[]{:S(2)}, u32[]{:S(2)}) async-start(bf16[1,2,640,4096]{3,1,0,2:T(2,128)(2,1)} %copy.50), calls=%async_computation.1 | async-start | bytes 20971520 | tf_op jit(solution)/shard_map/all_to_all | solution.py:89
  273.4 446.3 %all-reduce.5.cloned.1.call-start = ((), (), s32[]{:S(2)}) async-start(), calls=%async_computation.4 | async-start | bytes 524288 | tf_op jit(solution)/shard_map/psum | solution.py:107
  389.9 15.7 copy-start.26
  389.9 15.7 copy-start.29
  405.6 20.3 copy-start.11
  405.6 20.3 copy-start.15
  405.6 20.3 copy-start.19
  405.6 20.3 copy-start.17
  405.6 20.4 copy-start.5
  427.4 2105.9 %all-reduce.7.cloned.1.call-start = ((), (), s32[]{:S(2)}) async-start(), calls=%async_computation.5 | async-start | bytes 188743680 | tf_op jit(solution)/shard_map/psum | solution.py:108
  450.9 1.7 copy-start.7
  649.7 9.7 copy-start.9
  659.4 8.8 copy-start.2
  659.4 8.9 copy-start.13
  659.4 8.9 copy-start.21
  659.4 8.9 copy-start.23
  2534.9 50.1 %slice-start = ((s8[31457280]{0:T(1024)(128)(4,1)}), s8[4194304]{0:T(1024)(128)(4,1)S(1)}, s32[]{:S(2)}) async-start(s8[31457280]{0:T(1024)(128)(4,1)} %bitcast.55), calls=%async_computation.6 | async-start | bytes 8388608
  2534.9 50.1 %slice-start.1 = ((s8[31457280]{0:T(1024)(128)(4,1)}), s8[4194304]{0:T(1024)(128)(4,1)S(1)}, s32[]{:S(2)}) async-start(s8[31457280]{0:T(1024)(128)(4,1)} %bitcast.55), calls=%async_computation.7 | async-start | bytes 8388608
  2534.9 50.1 %slice-start.2 = ((s8[31457280]{0:T(1024)(128)(4,1)}), s8[4194304]{0:T(1024)(128)(4,1)S(1)}, s32[]{:S(2)}) async-start(s8[31457280]{0:T(1024)(128)(4,1)} %bitcast.55), calls=%async_computation.8 | async-start | bytes 8388608
  2534.9 50.1 %slice-start.3 = ((s8[31457280]{0:T(1024)(128)(4,1)}), s8[4194304]{0:T(1024)(128)(4,1)S(1)}, s32[]{:S(2)}) async-start(s8[31457280]{0:T(1024)(128)(4,1)} %bitcast.55), calls=%async_computation.9 | async-start | bytes 8388608
  2560.0 25.1 slice-start.4
  2560.0 25.1 slice-start.5
  2560.0 25.1 slice-start.6
  2560.0 25.1 slice-start.7
Sparse Core Ops, SparseCore 0:
  427.5 65.2 all-reduce.4
  496.1 2037.0 all-reduce.6
where the time goes:
time: 2610 us; the launch traced here: 2600 us
  waiting for transfers between devices  1980 us (76%)
  matrix products  252 us (10%)
  local copies, waits for them, and re-layouts  164 us (6%)
  blocking collectives  154 us (6%)
  other arithmetic  26.2 us (1%)
    psum x1, waiting for transfers between devices, local_step(): expert_sums = lax.psum((grad_gate, grad_up, grad_down), 'dp')  1810 us
    all_to_all x1, blocking collectives, local_step(): lax.all_to_all(d_expert_in.reshape(1, local_exp, n_ep * capacity, model_d...  120 us
    all_to_all x1, waiting for transfers between devices, local_step(): lax.all_to_all(send_rows.reshape(n_ep, local_exp, capacity, model_dim), '...  92.9 us
    unnamed x80, local copies, waits for them, and re-layouts  66.2 us
  transfers between devices with their start and end apart: 5, of which 4 were waited for; matrix products, arithmetic and copies ran while one was open for 12% of the time, Pallas kernels for 0%

commit v1 on v0

v1 whole, which is shorter than its diff:
```python
import jax
import jax.numpy as jnp
from jax import lax
from jax.experimental import pallas as pl
from jax.experimental.pallas import tpu as pltpu
from jax.sharding import PartitionSpec as P


LN_EPS = 1e-5
SWAP = [(0, 1), (1, 0)]


def capacity_for(tokens_dev, experts, n_top):
    return 8 * ((5 * tokens_dev * n_top + 32 * experts - 1) // (32 * experts))


def norm_forward(x_loc, ln_gain, ln_bias):
    x_f = x_loc.astype(jnp.float32)
    mean_x = jnp.mean(x_f, axis=-1, keepdims=True)
    centered = x_f - mean_x
    var_x = jnp.mean(centered * centered, axis=-1, keepdims=True)
    inv_std = lax.rsqrt(var_x + LN_EPS)
    normed = centered * inv_std
    hidden = (normed * ln_gain + ln_bias).astype(jnp.bfloat16)
    return x_f, hidden, normed, inv_std


def norm_backward(d_hidden, normed, inv_std, ln_gain):
    d_normed = d_hidden * ln_gain
    mean_dn = jnp.mean(d_normed, axis=-1, keepdims=True)
    mean_dnn = jnp.mean(d_normed * normed, axis=-1, keepdims=True)
    return inv_std * (d_normed - mean_dn - normed * mean_dnn)


def dot32(lhs, rhs, dims):
    return lax.dot_general(lhs, rhs, (dims, ((), ())), preferred_element_type=jnp.float32)


def acts(rows, gate_e, up_e):
    pre_gate = dot32(rows, gate_e, ((1,), (0,))).astype(jnp.bfloat16)
    pre_up = dot32(rows, up_e, ((1,), (0,))).astype(jnp.bfloat16)
    gate_f = pre_gate.astype(jnp.float32)
    act_mix = (gate_f * jax.nn.sigmoid(gate_f) * pre_up.astype(jnp.float32)).astype(jnp.bfloat16)
    return pre_gate, pre_up, act_mix


def act_grads(pre_gate, pre_up, grad_rows, down_e):
    d_mix = dot32(grad_rows, down_e, ((1,), (1,))).astype(jnp.bfloat16).astype(jnp.float32)
    gate_f = pre_gate.astype(jnp.float32)
    sig_gate = jax.nn.sigmoid(gate_f)
    up_f = pre_up.astype(jnp.float32)
    d_pre_gate = (d_mix * up_f * sig_gate * (1.0 + gate_f * (1.0 - sig_gate))).astype(jnp.bfloat16)
    d_pre_up = (d_mix * gate_f * sig_gate).astype(jnp.bfloat16)
    return d_pre_gate, d_pre_up


def row_sum_dot(lhs_a, rhs_a, lhs_b, rhs_b):
    dims = (((0,), (0,)), ((), ()))
    part = lax.dot_general(lhs_a, rhs_a, dims, preferred_element_type=jnp.float32)
    return part + lax.dot_general(lhs_b, rhs_b, dims, preferred_element_type=jnp.float32)


def weight_grad(expert, experts, cols_a, cols_b, rows_a, rows_b, prev, tile=512):
    n_rows, width = rows_a.shape
    inner = cols_a.shape[1]

    def body(*refs):
        ca, cb, ra, rb = refs[:4]
        refs[-1][0] = row_sum_dot(ca[...], ra[...], cb[...], rb[...])

    row_spec = pl.BlockSpec((n_rows, tile), lambda i: (0, i))
    full_spec = pl.BlockSpec((n_rows, inner), lambda i: (0, 0))
    return pl.pallas_call(
        body,
        grid=(width // tile,),
        in_specs=[full_spec, full_spec, row_spec, row_spec] + [pl.BlockSpec(memory_space=pl.ANY)] * len(prev),
        out_specs=pl.BlockSpec((1, inner, tile), lambda i: (expert, 0, i)),
        out_shape=jax.ShapeDtypeStruct((experts, inner, width), jnp.float32),
        input_output_aliases={4 + i: i for i in range(len(prev))},
        compiler_params=pltpu.CompilerParams(dimension_semantics=("arbitrary",), vmem_limit_bytes=40 * 2**20),
        cost_estimate=pl.CostEstimate(flops=4 * n_rows * width * inner, bytes_accessed=4 * n_rows * width + 4 * width * inner, transcendentals=0),
    )(cols_a, cols_b, rows_a, rows_b, *prev)


def sum_all(mesh_shape, rows):
    n_dp, n_ep = mesh_shape
    n_dev = n_dp * n_ep
    n, width = rows.shape
    cols = width // n_dev

    def body(in_ref, out_ref, got, mine, send_a, recv_a, send_b, recv_b):
        my_dp, my_ep = lax.axis_index("dp"), lax.axis_index("ep")
        me = my_dp * n_ep + my_ep
        barrier = pltpu.get_barrier_semaphore()

        def peer(k):
            other = lax.rem(me + k, n_dev)
            return other, (other // n_ep, lax.rem(other, n_ep))

        for k in range(1, n_dev):
            pl.semaphore_signal(barrier, inc=1, device_id=peer(k)[1], device_id_type=pl.DeviceIdType.MESH)
        pl.semaphore_wait(barrier, n_dev - 1)
        first = []
        for k in range(1, n_dev):
            other, dev = peer(k)
            copy = pltpu.make_async_remote_copy(
                src_ref=in_ref.at[:, pl.ds(pl.multiple_of(other * cols, 128), cols)], dst_ref=got.at[k],
                send_sem=send_a.at[k], recv_sem=recv_a.at[k], device_id=dev, device_id_type=pl.DeviceIdType.MESH)
            copy.start()
            first.append(copy)
        my_cols = pl.ds(pl.multiple_of(me * cols, 128), cols)
        total = in_ref[:, my_cols]
        for k in range(1, n_dev):
            first[k - 1].wait_recv()
            total = total + got[k]
        mine[...] = total
        out_ref[:, my_cols] = total
        for copy in first:
            copy.wait_send()
        second = []
        for k in range(1, n_dev):
            copy = pltpu.make_async_remote_copy(
                src_ref=mine, dst_ref=out_ref.at[:, my_cols],
                send_sem=send_b.at[k], recv_sem=recv_b.at[k], device_id=peer(k)[1], device_id_type=pl.DeviceIdType.MESH)
            copy.start()
            second.append(copy)
        for copy in second:
            copy.wait()

    return pl.pallas_call(
        body,
        in_specs=[pl.BlockSpec(memory_space=pltpu.VMEM)],
        out_specs=pl.BlockSpec(memory_space=pltpu.VMEM),
        out_shape=jax.ShapeDtypeStruct((n, width), jnp.float32),
        scratch_shapes=[pltpu.VMEM((n_dev, n, cols), jnp.float32), pltpu.VMEM((n, cols), jnp.float32)]
        + [pltpu.SemaphoreType.DMA((n_dev,))] * 4,
        compiler_params=pltpu.CompilerParams(collective_id=7, has_side_effects=True),
        name="sum_all",
    )(rows)


def solution(mesh):
    n_ep = mesh.shape["ep"]
    tok_spec = P(("dp", "ep"), None)
    exp_spec = P("ep", None, None)

    def local_step(x_loc, ln_gain, ln_bias, w_router, gate_loc, up_loc, down_loc, ids_loc, slots_loc, dout_loc):
        tokens_dev, model_dim = x_loc.shape
        experts = w_router.shape[1]
        local_exp = gate_loc.shape[0]
        n_top = ids_loc.shape[1]
        capacity = capacity_for(tokens_dev, experts, n_top)
        half = n_ep * capacity
        slot_rows = experts * capacity

        def exchange(rows):
            out = lax.all_to_all(rows.reshape(n_ep, capacity, model_dim), "ep", 0, 0, tiled=True)
            return out.reshape(half, model_dim)

        def swap(rows):
            return lax.ppermute(rows, "dp", SWAP)

        x_f, hidden, normed, inv_std = norm_forward(x_loc, ln_gain, ln_bias)
        pos = (ids_loc % local_exp) * half + (ids_loc // local_exp) * capacity + slots_loc
        pos = jnp.where(slots_loc >= 0, pos, -1)
        row_ids = jnp.arange(slot_rows)
        pair_hit = row_ids[:, None, None] == pos.T[None, :, :]
        row_hot = jnp.any(pair_hit, axis=1).astype(jnp.bfloat16)

        h_own, h_oth, g_own, g_oth = [], [], [], []
        for le in range(local_exp):
            rows = dot32(row_hot[le * half : (le + 1) * half], hidden, ((1,), (0,))).astype(jnp.bfloat16)
            h_own.append(exchange(rows))
            h_oth.append(swap(h_own[le]))

        logits = jnp.dot(hidden, w_router, preferred_element_type=jnp.float32)
        pick_mask = (ids_loc[..., None] == jnp.arange(experts)).astype(jnp.float32)
        gate_probs = jax.nn.softmax(jnp.sum(pick_mask * logits[..., None, :], axis=-1), axis=-1)
        row_prob = jnp.sum(jnp.where(pair_hit, gate_probs.T[None, :, :], 0.0), axis=(1, 2))
        for le in range(local_exp):
            part = slice(le * half, (le + 1) * half)
            rows = (dot32(row_hot[part], dout_loc, ((1,), (0,))) * row_prob[part, None]).astype(jnp.bfloat16)
            g_own.append(exchange(rows))
            g_oth.append(swap(g_own[le]))

        y_ret, d_ret, saved = [], [], []
        for le in range(local_exp):
            pre_gate, pre_up, act_mix = acts(h_own[le], gate_loc[le], up_loc[le])
            y_rows = dot32(act_mix, down_loc[le], ((1,), (0,))).astype(jnp.bfloat16)
            y_ret.append(exchange(y_rows))
            saved.append((pre_gate, pre_up, act_mix))
        own = []
        for le in range(local_exp):
            pre_gate, pre_up, act_mix = saved[le]
            dg, du = act_grads(pre_gate, pre_up, g_own[le], down_loc[le])
            d_rows = (dot32(dg, gate_loc[le], ((1,), (1,))) + dot32(du, up_loc[le], ((1,), (1,)))).astype(jnp.bfloat16)
            d_ret.append(exchange(d_rows))
            own.append((act_mix, dg, du))
        grads = [(), (), ()]
        for le in range(local_exp):
            mix_own, dg_own, du_own = own[le]
            pre_gate, pre_up, mix_oth = acts(h_oth[le], gate_loc[le], up_loc[le])
            dg_oth, du_oth = act_grads(pre_gate, pre_up, g_oth[le], down_loc[le])
            cols = ((dg_own, dg_oth, h_own[le], h_oth[le]), (du_own, du_oth, h_own[le], h_oth[le]), (mix_own, mix_oth, g_own[le], g_oth[le]))
            grads = [weight_grad(le, local_exp, *cols[n], grads[n]) for n in range(3)]
            grads = [(g,) for g in grads]

        ret_rows = jnp.concatenate(y_ret, axis=0)
        pair_hot = (pos[..., None] == row_ids).astype(jnp.bfloat16)
        pair_out = jnp.dot(pair_hot.reshape(tokens_dev * n_top, slot_rows), ret_rows, preferred_element_type=jnp.float32)
        pair_out = pair_out.reshape(tokens_dev, n_top, model_dim)
        moe_out = (x_f + jnp.sum(gate_probs[..., None] * pair_out, axis=1)).astype(jnp.bfloat16)
        dout_f = dout_loc.astype(jnp.float32)
        d_gates = jnp.sum(pair_out * dout_f[:, None, :], axis=-1)
        d_chosen = gate_probs * (d_gates - jnp.sum(gate_probs * d_gates, axis=-1, keepdims=True))
        d_logits = jnp.sum(d_chosen[..., None] * pick_mask, axis=-2)

        d_hidden_moe = dot32(row_hot, jnp.concatenate(d_ret, axis=0), ((0,), (0,)))
        d_hidden_router = jnp.einsum("te,me->tm", d_logits, w_router, preferred_element_type=jnp.float32)
        d_hidden = (d_hidden_moe + d_hidden_router).astype(jnp.bfloat16).astype(jnp.float32)
        grad_x = (dout_f + norm_backward(d_hidden, normed, inv_std, ln_gain)).astype(jnp.bfloat16)
        router_part = dot32(d_logits, hidden.astype(jnp.float32), ((0,), (0,)))
        norm_part = jnp.stack([jnp.sum(d_hidden * normed, axis=0), jnp.sum(d_hidden, axis=0)])
        pad = jnp.zeros((-(experts + 2) % 8, model_dim), jnp.float32)
        sums = sum_all((mesh.shape["dp"], n_ep), jnp.concatenate([router_part, norm_part, pad], axis=0))
        grad_gate, grad_up = (jnp.swapaxes(g[0], 1, 2) for g in grads[:2])
        return moe_out, grad_x, sums[experts], sums[experts + 1], sums[:experts].T, grad_gate, grad_up, grads[2][0]

    return jax.shard_map(local_step, mesh=mesh, in_specs=(tok_spec, P(None), P(None), P(None, None), exp_spec, exp_spec, exp_spec, tok_spec, tok_spec, tok_spec), out_specs=(tok_spec, tok_spec, P(None), P(None), P(None, None), exp_spec, exp_spec, exp_spec), check_vma=False)
```

time: 2610 us -> 1150 us (0.44)
  waiting for transfers between devices: 1980 us -> 310 us
  Pallas kernels: 0 us -> 500 us
  blocking collectives: 154 us -> 0 us
  local copies, waits for them, and re-layouts: 164 us -> 12.1 us
  starting transfers between devices: 16.1 us -> 43.7 us
    psum x2 -> x0, waiting for transfers between devices: 1810 us -> none  [the longest x1 1810 us: local_step(): expert_sums = lax.psum((grad_gate, grad_up, grad_down), 'dp')]
    pallas_call x0 -> x7, Pallas kernels: none -> 500 us  [the longest x1 396 us: sum_all(): pl.pallas_call(body, in_specs=[pl.BlockSpec(memory_space=pltpu.VMEM)], ou...]
    all_to_all x3 -> x8, waiting for transfers between devices: 163 us -> 310 us  [exchange(): lax.all_to_all(rows.reshape(n_ep, capacity, model_dim), 'ep', 0, 0, tiled...]
    all_to_all x1 -> x0, blocking collectives: 120 us -> none  [local_step(): lax.all_to_all(d_expert_in.reshape(1, local_exp, n_ep * capacity, model_d...]
    unnamed x80 -> x88, local copies, waits for them, and re-layouts: 66.2 us -> 3.78 us
    all_to_all x5 -> x0, local copies, waits for them, and re-layouts: 60.2 us -> none  [the longest x2 25.1 us: local_step(): lax.all_to_all(d_expert_in.reshape(1, local_exp, n_ep * capacity, model_d...]
    reshape x2 -> x0, local copies, waits for them, and re-layouts: 37.9 us -> none  [the longest x1 20 us: local_step(): expert_out.reshape(1, local_exp, n_ep * capacity, model_dim)]
    psum x1 -> x0, blocking collectives: 34.2 us -> none  [local_step(): lax.psum((jnp.sum(d_hidden * normed, axis=0), jnp.sum(d_hidden, axis=0),...]
  transfers between devices with their start and end apart: 5 -> 12, of which waited for: 4 -> 8; matrix products, arithmetic and copies ran while one was open for 12% -> 21% of each run, Pallas kernels for 0% -> 35%
where the time goes in v1:
time: 1150 us; the launch traced here: 1140 us
  Pallas kernels  500 us (43%)
  waiting for transfers between devices  310 us (27%)
  matrix products  248 us (22%)
  starting transfers between devices  43.7 us (4%)
  other arithmetic  27.8 us (2%)
  local copies, waits for them, and re-layouts  12.1 us (1%)
    pallas_call x1, Pallas kernels, sum_all(): pl.pallas_call(body, in_specs=[pl.BlockSpec(memory_space=pltpu.VMEM)], ou...  396 us
    all_to_all x8, waiting for transfers between devices, exchange(): lax.all_to_all(rows.reshape(n_ep, capacity, model_dim), 'ep', 0, 0, tiled...  310 us
    dot_general x24, matrix products, dot32(): lax.dot_general(lhs, rhs, (dims, ((), ())), preferred_element_type=jnp.fl...  221 us
    pallas_call x6, Pallas kernels, weight_grad(): pl.pallas_call(body, grid=(width // tile,), in_specs=[full_spec, full_spe...  104 us
    all_to_all x8, starting transfers between devices, exchange(): lax.all_to_all(rows.reshape(n_ep, capacity, model_dim), 'ep', 0, 0, tiled...  39.3 us
  transfers between devices with their start and end apart: 12, of which 8 were waited for; matrix products, arithmetic and copies ran while one was open for 21% of the time, Pallas kernels for 35%

profile of v1, /device:TPU:0, one launch (start us, length us, event | category | flops | bytes accessed | tf_op | source)
XLA Modules:
  0.0 1143.1 jit_solution(16209952461287063282)
XLA Ops:
  13.2 6.8 multiply_convert_fusion
  20.0 5.4 all-to-all-start.6
  25.4 6.8 convolution_convert_fusion
  32.2 53.7 %all-to-all-done.6 = bf16[8,80,4096]{2,1,0:T(8,128)(2,1)} async-done(((bf16[8,80,4096]{2,1,0:T(8,128)(2,1)}), bf16[8,80,4096]{2,1,0:T(8,128)(2,1)}, u32[]{:S(2)}, u32[]{:S(2)}) %all-to-all-start.6) | async-done | bytes 5242912 | tf_op jit(solution)/shard_map/all_to_all | solution.py:157
  90.6 6.8 multiply_convert_fusion.1
  97.3 53.6 %all-to-all-done.2 = bf16[8,80,4096]{2,1,0:T(8,128)(2,1)} async-done(((bf16[8,80,4096]{2,1,0:T(8,128)(2,1)}), bf16[8,80,4096]{2,1,0:T(8,128)(2,1)}, u32[]{:S(2)}, u32[]{:S(2)}) %all-to-all-start.2) | async-done | bytes 5242912 | tf_op jit(solution)/shard_map/all_to_all | solution.py:157
  150.9 4.8 all-to-all-start.4
  155.8 6.9 convolution_convert_fusion.1
  162.7 10.0 fusion.157
  172.8 8.8 fusion.145
  181.6 34.5 %all-to-all-done.4 = bf16[8,80,4096]{2,1,0:T(8,128)(2,1)} async-done(((bf16[8,80,4096]{2,1,0:T(8,128)(2,1)}), bf16[8,80,4096]{2,1,0:T(8,128)(2,1)}, u32[]{:S(2)}, u32[]{:S(2)}) %all-to-all-start.4) | async-done | bytes 5242912 | tf_op jit(solution)/shard_map/all_to_all | solution.py:157
  216.1 4.9 all-to-all-start
  221.0 12.3 %fusion.96 = (bf16[640,960]{1,0:T(8,128)(2,1)}, bf16[640,960]{1,0:T(8,128)(2,1)}, bf16[640,960]{1,0:T(8,128)(2,1)S(1)}) fusion(bf16[640,960]{1,0:T(8,128)(2,1)S(1)} %fusion.157, bf16[640,960]{1,0:T(8,128)(2,1)} %fusion.145, bf16[640,4096]{1,0:T(8,128)(2,1)} %bitcast.9.refs_2_, bf16[2,4096,960]{1,2,0:T(8,128)(2,1)} %param.15), kind=kOutput, calls=%fused_computation.131 | convolution fusion | flops 5045452800 | bytes 19333120 | tf_op jit(solution)/shard_map/dot_general | solution.py:36
  233.3 11.0 fusion.63
  244.3 8.5 fusion.142
  252.8 28.5 %all-to-all-done = bf16[8,80,4096]{2,1,0:T(8,128)(2,1)} async-done(((bf16[8,80,4096]{2,1,0:T(8,128)(2,1)}), bf16[8,80,4096]{2,1,0:T(8,128)(2,1)}, u32[]{:S(2)}, u32[]{:S(2)}) %all-to-all-start) | async-done | bytes 5242912 | tf_op jit(solution)/shard_map/all_to_all | solution.py:157
  281.3 4.9 all-to-all-start.3
  286.2 10.0 fusion.130
  296.2 10.9 fusion.93
  307.1 10.5 fusion.60
  318.7 27.9 %all-to-all-done.3 = bf16[8,80,4096]{2,1,0:T(8,128)(2,1)} async-done(((bf16[8,80,4096]{2,1,0:T(8,128)(2,1)}), bf16[8,80,4096]{2,1,0:T(8,128)(2,1)}, u32[]{:S(2)}, u32[]{:S(2)}) %all-to-all-start.3) | async-done | bytes 5242912 | tf_op jit(solution)/shard_map/all_to_all | solution.py:157
  346.6 5.1 all-to-all-start.1
  351.7 7.9 fusion.50
  359.6 10.7 add_convert_fusion.1
  370.4 41.7 %all-to-all-done.1 = bf16[8,80,4096]{2,1,0:T(8,128)(2,1)} async-done(((bf16[8,80,4096]{2,1,0:T(8,128)(2,1)}), bf16[8,80,4096]{2,1,0:T(8,128)(2,1)}, u32[]{:S(2)}, u32[]{:S(2)}) %all-to-all-start.1) | async-done | bytes 5242912 | tf_op jit(solution)/shard_map/all_to_all | solution.py:157
  416.7 8.4 fusion.32
  425.2 10.8 add_convert_fusion
  435.9 41.1 %all-to-all-done.5 = bf16[8,80,4096]{2,1,0:T(8,128)(2,1)} async-done(((bf16[8,80,4096]{2,1,0:T(8,128)(2,1)}), bf16[8,80,4096]{2,1,0:T(8,128)(2,1)}, u32[]{:S(2)}, u32[]{:S(2)}) %all-to-all-start.5) | async-done | bytes 5242912 | tf_op jit(solution)/shard_map/all_to_all | solution.py:157
  477.1 4.8 all-to-all-start.7
  481.9 6.7 convert_element_type.182
  493.1 19.7 %multiply_reduce_fusion = (f32[512,2]{0,1:T(2,128)S(1)}, f32[512,4096]{1,0:T(8,128)}) fusion(f32[512,4096]{1,0:T(8,128)} %convert_element_type.182, f32[512,2]{0,1:T(2,128)S(1)} %fusion.173, bf16[640,4096]{1,0:T(8,128)(2,1)} %bitcast.14, bf16[640,4096]{1,0:T(8,128)(2,1)} %bitcast.7, s32[512,2]{0,1:T(2,128)S(1)} %copy-done.26), kind=kOutput, calls=%fused_computation | convolution fusion | flops 10774379520 | bytes 27275264 | tf_op jit(solution)/shard_map/dot_general | solution.py:210
  513.0 29.2 %all-to-all-done.7 = bf16[8,80,4096]{2,1,0:T(8,128)(2,1)} async-done(((bf16[8,80,4096]{2,1,0:T(8,128)(2,1)}), bf16[8,80,4096]{2,1,0:T(8,128)(2,1)}, u32[]{:S(2)}, u32[]{:S(2)}) %all-to-all-start.7) | async-done | bytes 5242912 | tf_op jit(solution)/shard_map/all_to_all | solution.py:157
  542.2 9.0 fusion.6
  551.3 5.6 fusion.23
  558.4 395.6 %sum_all.1 = f32[24,4096]{1,0:T(8,128)} custom-call(f32[24,4096]{1,0:T(8,128)} %maximum_maximum_fusion.in_ref), custom_call_target="tpu_custom_call" | custom-call | tf_op jit(solution)/shard_map/sum_all/pallas_call | solution.py:130
  955.8 11.6 %fusion.19 = (bf16[512,4096]{1,0:T(8,128)(2,1)}, bf16[512,4096]{1,0:T(8,128)(2,1)}) fusion(bf16[512,4096]{1,0:T(8,128)(2,1)} %param.10, bf16[512,4096]{1,0:T(8,128)(2,1)} %get-tuple-element.32, f32[512]{0:T(512)S(1)} %get-tuple-element.33, f32[512]{0:T(512)S(1)} %get-tuple-element.34, f32[4096]{0:T(1024)S(1)} %copy-done.22, f32[512]{0:T(512)S(1)} %copy-done.32, ...), kind=kLoop, calls=%fused_computation.32 | loop fusion | flops 29360128 | bytes 29384704 | tf_op jit(solution)/shard_map/convert_element_type | solution.py:221
  969.0 11.0 fusion.163
  982.5 11.0 fusion.160
  996.0 10.3 fusion.133
  1006.2 10.0 fusion.148
  1016.2 11.0 fusion.104
  1027.2 17.4 %shard_map.165.refs_4_ = f32[2,960,4096]{2,1,0:T(8,128)} custom-call(bf16[640,960]{1,0:T(8,128)(2,1)S(1)} %copy-done.3, bf16[640,960]{1,0:T(8,128)(2,1)S(1)} %get-tuple-element.16.refs_1_, bf16[640,4096]{1,0:T(8,128)(2,1)} %bitcast.18.refs_2_, bf16[640,4096]{1,0:T(8,128)(2,1)} %collective-permute-done.2.refs_3_), custom_call_target="tpu_custom_call" | custom-call | flops 10066329600 | bytes 26214400 | tf_op jit(solution)/shard_map/pallas_call | solution.py:73
  1044.6 17.4 %shard_map.161.refs_4_ = f32[2,960,4096]{2,1,0:T(8,128)} custom-call(bf16[640,960]{1,0:T(8,128)(2,1)S(1)} %get-tuple-element.22.refs_0_, bf16[640,960]{1,0:T(8,128)(2,1)S(1)} %get-tuple-element.17.refs_1_, bf16[640,4096]{1,0:T(8,128)(2,1)} %bitcast.2.refs_2_, bf16[640,4096]{1,0:T(8,128)(2,1)} %collective-permute-done.3.refs_3_), custom_call_target="tpu_custom_call" | custom-call | flops 10066329600 | bytes 26214400 | tf_op jit(solution)/shard_map/pallas_call | solution.py:73
  1061.9 17.5 %shard_map.163.refs_4_ = f32[2,960,4096]{2,1,0:T(8,128)} custom-call(bf16[640,960]{1,0:T(8,128)(2,1)S(1)} %get-tuple-element.23.refs_0_, bf16[640,960]{1,0:T(8,128)(2,1)S(1)} %get-tuple-element.18.refs_1_, bf16[640,4096]{1,0:T(8,128)(2,1)} %bitcast.2.refs_2_, bf16[640,4096]{1,0:T(8,128)(2,1)} %collective-permute-done.3.refs_3_), custom_call_target="tpu_custom_call" | custom-call | flops 10066329600 | bytes 26214400 | tf_op jit(solution)/shard_map/pallas_call | solution.py:73
  1079.4 11.1 fusion.100
  1090.6 17.5 %shard_map.166 = f32[2,960,4096]{2,1,0:T(8,128)} custom-call(bf16[640,960]{1,0:T(8,128)(2,1)S(1)} %copy-done.8, bf16[640,960]{1,0:T(8,128)(2,1)S(1)} %get-tuple-element.19.refs_1_, bf16[640,4096]{1,0:T(8,128)(2,1)} %bitcast.22.refs_2_, bf16[640,4096]{1,0:T(8,128)(2,1)} %collective-permute-done.refs_3_, ...), custom_call_target="tpu_custom_call", output_to_operand_aliasing={{}: (4, {})} | custom-call | flops 10066329600 | bytes 26214400 | tf_op jit(solution)/shard_map/pallas_call | solution.py:73
  1108.1 17.5 %shard_map.162 = f32[2,960,4096]{2,1,0:T(8,128)} custom-call(bf16[640,960]{1,0:T(8,128)(2,1)S(1)} %copy-done.6, bf16[640,960]{1,0:T(8,128)(2,1)S(1)} %get-tuple-element.20.refs_1_, bf16[640,4096]{1,0:T(8,128)(2,1)} %bitcast.9.refs_2_, bf16[640,4096]{1,0:T(8,128)(2,1)} %collective-permute-done.1.refs_3_, ...), custom_call_target="tpu_custom_call", output_to_operand_aliasing={{}: (4, {})} | custom-call | flops 10066329600 | bytes 26214400 | tf_op jit(solution)/shard_map/pallas_call | solution.py:73
  1125.5 17.4 %shard_map.164 = f32[2,960,4096]{2,1,0:T(8,128)} custom-call(bf16[640,960]{1,0:T(8,128)(2,1)S(1)} %copy-done.4, bf16[640,960]{1,0:T(8,128)(2,1)S(1)} %get-tuple-element.21.refs_1_, bf16[640,4096]{1,0:T(8,128)(2,1)} %bitcast.9.refs_2_, bf16[640,4096]{1,0:T(8,128)(2,1)} %collective-permute-done.1.refs_3_, ...), custom_call_target="tpu_custom_call", output_to_operand_aliasing={{}: (4, {})} | custom-call | flops 10066329600 | bytes 26214400 | tf_op jit(solution)/shard_map/pallas_call | solution.py:73
  (127 shorter events, 37.2 us)
Async XLA Ops:
  0.6 10.6 copy-start
  0.7 6.2 copy-start.21
  0.7 6.2 copy-start.33
  5.4 7.1 copy-start.25
  6.9 148.8 %copy-start.15 = (pred[1280,512]{1,0:T(8,128)(4,1)}, pred[1280,512]{1,0:T(8,128)(4,1)S(1)}, u32[]{:S(2)}) copy-start(pred[1280,512]{1,0:T(8,128)(4,1)S(1)} %fusion.88) | copy-start | bytes 1966084
  12.4 7.5 copy-start.17
  12.5 7.5 copy-start.19
  12.5 7.5 copy-start.23
  20.0 65.9 %all-to-all-start.6 = ((bf16[8,80,4096]{2,1,0:T(8,128)(2,1)}), bf16[8,80,4096]{2,1,0:T(8,128)(2,1)}, u32[]{:S(2)}, u32[]{:S(2)}) async-start(bf16[8,80,4096]{2,1,0:T(8,128)(2,1)} %bitcast.152), calls=%async_computation.6 | async-start | bytes 10485760 | tf_op jit(solution)/shard_map/all_to_all | solution.py:157
  85.9 65.0 %all-to-all-start.2 = ((bf16[8,80,4096]{2,1,0:T(8,128)(2,1)}), bf16[8,80,4096]{2,1,0:T(8,128)(2,1)}, u32[]{:S(2)}, u32[]{:S(2)}) async-start(bf16[8,80,4096]{2,1,0:T(8,128)(2,1)} %bitcast.151), calls=%async_computation.2 | async-start | bytes 10485760 | tf_op jit(solution)/shard_map/all_to_all | solution.py:157
  150.9 65.2 %all-to-all-start.4 = ((bf16[8,80,4096]{2,1,0:T(8,128)(2,1)}), bf16[8,80,4096]{2,1,0:T(8,128)(2,1)}, u32[]{:S(2)}, u32[]{:S(2)}) async-start(bf16[8,80,4096]{2,1,0:T(8,128)(2,1)} %bitcast.149), calls=%async_computation.4 | async-start | bytes 10485760 | tf_op jit(solution)/shard_map/all_to_all | solution.py:157
  155.7 17.0 %slice-start.4 = ((s8[15728640]{0:T(1024)(128)(4,1)}), s8[4194304]{0:T(1024)(128)(4,1)S(1)}, s32[]{:S(2)}) async-start(s8[15728640]{0:T(1024)(128)(4,1)} %bitcast.161), calls=%async_computation.12 | async-start | bytes 8388608
  155.8 17.0 %slice-start.5 = ((s8[15728640]{0:T(1024)(128)(4,1)}), s8[4194304]{0:T(1024)(128)(4,1)S(1)}, s32[]{:S(2)}) async-start(s8[15728640]{0:T(1024)(128)(4,1)} %bitcast.161), calls=%async_computation.13 | async-start | bytes 8388608
  162.7 10.0 slice-start.6
  162.7 10.0 slice-start.7
  216.1 65.2 %all-to-all-start = ((bf16[8,80,4096]{2,1,0:T(8,128)(2,1)}), bf16[8,80,4096]{2,1,0:T(8,128)(2,1)}, u32[]{:S(2)}, u32[]{:S(2)}) async-start(bf16[8,80,4096]{2,1,0:T(8,128)(2,1)} %bitcast.146), calls=%async_computation | async-start | bytes 10485760 | tf_op jit(solution)/shard_map/all_to_all | solution.py:157
  221.0 23.3 %slice-start = ((s8[15728640]{0:T(1024)(128)(4,1)}), s8[3145728]{0:T(1024)(128)(4,1)S(1)}, s32[]{:S(2)}) async-start(s8[15728640]{0:T(1024)(128)(4,1)} %bitcast.159), calls=%async_computation.8 | async-start | bytes 6291456
  221.0 23.3 %slice-start.1 = ((s8[15728640]{0:T(1024)(128)(4,1)}), s8[4194304]{0:T(1024)(128)(4,1)S(1)}, s32[]{:S(2)}) async-start(s8[15728640]{0:T(1024)(128)(4,1)} %bitcast.159), calls=%async_computation.9 | async-start | bytes 8388608
  221.0 23.3 %slice-start.2 = ((s8[15728640]{0:T(1024)(128)(4,1)}), s8[4194304]{0:T(1024)(128)(4,1)S(1)}, s32[]{:S(2)}) async-start(s8[15728640]{0:T(1024)(128)(4,1)} %bitcast.159), calls=%async_computation.10 | async-start | bytes 8388608
  233.3 11.0 copy-start.7
  233.3 11.0 slice-start.3
  281.3 65.3 %all-to-all-start.3 = ((bf16[8,80,4096]{2,1,0:T(8,128)(2,1)}), bf16[8,80,4096]{2,1,0:T(8,128)(2,1)}, u32[]{:S(2)}, u32[]{:S(2)}) async-start(bf16[8,80,4096]{2,1,0:T(8,128)(2,1)} %bitcast.147), calls=%async_computation.3 | async-start | bytes 10485760 | tf_op jit(solution)/shard_map/all_to_all | solution.py:157
  286.2 10.0 copy-start.35
  346.6 65.5 %all-to-all-start.1 = ((bf16[8,80,4096]{2,1,0:T(8,128)(2,1)}), bf16[8,80,4096]{2,1,0:T(8,128)(2,1)}, u32[]{:S(2)}, u32[]{:S(2)}) async-start(bf16[8,80,4096]{2,1,0:T(8,128)(2,1)} %bitcast.150), calls=%async_computation.1 | async-start | bytes 10485760 | tf_op jit(solution)/shard_map/all_to_all | solution.py:157
  412.1 65.0 %all-to-all-start.5 = ((bf16[8,80,4096]{2,1,0:T(8,128)(2,1)}), bf16[8,80,4096]{2,1,0:T(8,128)(2,1)}, u32[]{:S(2)}, u32[]{:S(2)}) async-start(bf16[8,80,4096]{2,1,0:T(8,128)(2,1)} %bitcast.148), calls=%async_computation.5 | async-start | bytes 10485760 | tf_op jit(solution)/shard_map/all_to_all | solution.py:157
  416.7 8.4 copy-start.5
  477.1 65.1 %all-to-all-start.7 = ((bf16[8,80,4096]{2,1,0:T(8,128)(2,1)}), bf16[8,80,4096]{2,1,0:T(8,128)(2,1)}, u32[]{:S(2)}, u32[]{:S(2)}) async-start(bf16[8,80,4096]{2,1,0:T(8,128)(2,1)} %bitcast.145), calls=%async_computation.7 | async-start | bytes 10485760 | tf_op jit(solution)/shard_map/all_to_all | solution.py:157
  481.9 6.8 copy-start.18
  481.9 6.8 copy-start.20
  481.9 6.8 copy-start.24
  481.9 11.2 copy-start.26
  488.7 507.3 %collective-permute-start.3 = (bf16[640,4096]{1,0:T(8,128)(2,1)}, bf16[640,4096]{1,0:T(8,128)(2,1)}, u32[]{:S(2)}, u32[]{:S(2)}) collective-permute-start(bf16[640,4096]{1,0:T(8,128)(2,1)} %bitcast.2.refs_2_), channel_id=1, source_target_pairs={{0,8},{8,0},{1,9},{9,1},{2,10},{10,2},{3,11},{11,3},{4,12},{12,4},... | collective-permute-start | bytes 15728648 | tf_op jit(solution)/shard_map/ppermute | solution.py:161
  491.1 515.2 %collective-permute-start.1 = (bf16[640,4096]{1,0:T(8,128)(2,1)}, bf16[640,4096]{1,0:T(8,128)(2,1)}, u32[]{:S(2)}, u32[]{:S(2)}) collective-permute-start(bf16[640,4096]{1,0:T(8,128)(2,1)} %bitcast.9.refs_2_), channel_id=1, source_target_pairs={{0,8},{8,0},{1,9},{9,1},{2,10},{10,2},{3,11},{11,3},{4,12},{12,4},... | collective-permute-start | bytes 15728648 | tf_op jit(solution)/shard_map/ppermute | solution.py:161
  491.1 477.9 %collective-permute-start = (bf16[640,4096]{1,0:T(8,128)(2,1)}, bf16[640,4096]{1,0:T(8,128)(2,1)}, u32[]{:S(2)}, u32[]{:S(2)}) collective-permute-start(bf16[640,4096]{1,0:T(8,128)(2,1)} %bitcast.22.refs_2_), channel_id=1, source_target_pairs={{0,8},{8,0},{1,9},{9,1},{2,10},{10,2},{3,11},{11,3},{4,12},{12,4},... | collective-permute-start | bytes 15728648 | tf_op jit(solution)/shard_map/ppermute | solution.py:161
  493.1 489.4 %collective-permute-start.2 = (bf16[640,4096]{1,0:T(8,128)(2,1)}, bf16[640,4096]{1,0:T(8,128)(2,1)}, u32[]{:S(2)}, u32[]{:S(2)}) collective-permute-start(bf16[640,4096]{1,0:T(8,128)(2,1)} %bitcast.18.refs_2_), channel_id=1, source_target_pairs={{0,8},{8,0},{1,9},{9,1},{2,10},{10,2},{3,11},{11,3},{4,12},{12,4},... | collective-permute-start | bytes 15728648 | tf_op jit(solution)/shard_map/ppermute | solution.py:161
  493.1 19.8 %copy-start.28 = (s32[512,2]{0,1:T(2,128)S(1)}, s32[512,2]{0,1:T(2,128)}, u32[]{:S(2)}) copy-start(s32[512,2]{0,1:T(2,128)} %param.17) | copy-start | bytes 12292
  493.1 49.1 %copy-start.16 = (pred[1280,512]{1,0:T(8,128)(4,1)S(1)}, pred[1280,512]{1,0:T(8,128)(4,1)}, u32[]{:S(2)}) copy-start(pred[1280,512]{1,0:T(8,128)(4,1)} %copy-done.15) | copy-start | bytes 1966084
  542.2 9.0 copy-start.10
  542.2 9.1 copy-start.22
  542.2 9.1 copy-start.30
  542.2 9.1 copy-start.32
  1006.2 10.0 copy-start.14
  1016.2 11.0 copy-start.3
  1061.9 17.5 %copy-start.13 = (bf16[640,960]{1,0:T(8,128)(2,1)S(1)}, bf16[640,960]{1,0:T(8,128)(2,1)}, u32[]{:S(2)}) copy-start(bf16[640,960]{1,0:T(8,128)(2,1)} %copy.54) | copy-start | bytes 3686404
  1079.4 11.2 copy-start.8
  1090.6 17.5 %copy-start.6 = (bf16[640,960]{1,0:T(8,128)(2,1)S(1)}, bf16[640,960]{1,0:T(8,128)(2,1)}, u32[]{:S(2)}) copy-start(bf16[640,960]{1,0:T(8,128)(2,1)} %get-tuple-element.25.refs_0_) | copy-start | bytes 3686404
  1108.1 17.5 %copy-start.4 = (bf16[640,960]{1,0:T(8,128)(2,1)S(1)}, bf16[640,960]{1,0:T(8,128)(2,1)}, u32[]{:S(2)}) copy-start(bf16[640,960]{1,0:T(8,128)(2,1)} %get-tuple-element.26.refs_0_) | copy-start | bytes 3686404
  1125.5 17.4 %copy-start.1 = (bf16[4096,16]{0,1:T(8,128)(2,1)S(1)}, bf16[4096,16]{0,1:T(8,128)(2,1)}, u32[]{:S(2)}) copy-start(bf16[4096,16]{0,1:T(8,128)(2,1)} %param.13) | copy-start | bytes 393220
  (8 other events, 25.9 us)
